TPU v7x, 32 devices: a whole 2x2x4 slice. The times are simulated.
32 devices in a mesh: patch: 8 (over z, x), member: 4 (over y, core).
Axes of the slice: x: 2, y: 2, z: 4, core: 2. Of those that a mesh axis runs over, the one named last changes fastest.
Arguments:
- background: bfloat16 [32, 16, 3, 64, 128], P('patch', None, None, 'member'), may hold values from -6 to 6
- patch_blocks: int32 [32], replicated, may hold values from 1 to 16, as said below
- obs_values: float32 [16384], P(('patch', 'member')), may hold values from -12 to 12
- obs_errors: float32 [16384], P(('patch', 'member')), may hold values from 0.5 to 2
- obs_patch: int32 [16384], P('patch'), may hold values from 0 to 3
- obs_position: int32 [16384], P('patch'), may hold values from 0 to 1073741823
Outputs:
- analysis: bfloat16 [32, 16, 3, 64, 128], P('patch', None, None, 'member')
- inflation: float32 [], replicated
Inputs may be any that keep to these rules, and one draw needn't show every extreme that they name: `obs_patch`: index among the 4 patches held by the observation's index of patch. `patch_blocks`: the used blocks of the 4 patches of one index of patch sum to at most 32; some index reaches 32, and some patch uses all 16.
All inputs are finite; a program needn't handle non-finite values.
Results may differ from a plain program's by a relative error of at most 0.0065.
Values may be sent and summed in bfloat16 or wider, within the bound.
A program may use at most 64 MiB of HBM per device.

v0:
```python
import math
import jax
import jax.numpy as jnp
from jax import lax
from jax.sharding import PartitionSpec as P

K = 64
CB = 128
MAXB = 16
NS_STEPS = 4
PD = 4
OBS_DEV = 2048
neighbour_weight = 0.5


def extended(array, sides, width):
    for axis, dim in sides:
        count, length = (lax.axis_size(axis), array.shape[dim])
        up = [(i, (i + 1) % count) for i in range(count - 1)]
        down = [(j, i) for i, j in up]
        last = lax.slice_in_dim(array, length - width, length, axis=dim)
        initial = lax.slice_in_dim(array, 0, width, axis=dim)
        before = lax.ppermute(last, axis, up)
        after = lax.ppermute(initial, axis, down)
        array = jnp.concatenate([before, array, after], axis=dim)
    return array


def inverse_root(system):
    precise = lax.Precision.HIGHEST
    identity = jnp.eye(K, dtype=jnp.float32)
    norm_value = jnp.sqrt(jnp.sum(system * system, axis=(1, 2)))
    square_part = system / norm_value[:, None, None]
    inverse_part = jnp.broadcast_to(identity, system.shape)
    for sweep_index in range(NS_STEPS):
        middle = 1.5 * identity - 0.5 * jnp.einsum(
            "pij,pjk->pik", inverse_part, square_part, precision=precise
        )
        square_part = jnp.einsum("pij,pjk->pik", square_part, middle, precision=precise)
        inverse_part = jnp.einsum("pij,pjk->pik", middle, inverse_part, precision=precise)
    return inverse_part / jnp.sqrt(norm_value)[:, None, None]


def per_device(background, patch_blocks, obs_values, obs_errors, obs_patch, obs_position):
    precise = lax.Precision.HIGHEST
    member_count = lax.axis_size("member")
    local_members = K // member_count
    obs_share = OBS_DEV // member_count
    block_share = MAXB // member_count
    member_index = lax.axis_index("member")
    first_patch = lax.axis_index("patch") * PD
    used_blocks = lax.dynamic_slice_in_dim(patch_blocks, first_patch, PD)
    slot_table = jnp.arange(PD, dtype=jnp.int32)
    onehot_all = obs_patch[None, :] == slot_table[:, None]
    obs_counts = jnp.sum(jnp.where(onehot_all, used_blocks[:, None], 0), axis=0)
    cell_index = obs_position % (obs_counts * CB)
    flat_index = obs_patch * (MAXB * CB) + cell_index
    thickness = jnp.transpose(background[:, :, 0], (0, 1, 3, 2)).reshape(
        PD * MAXB * CB, local_members
    )
    sampled_local = thickness[flat_index]
    sampled = lax.all_to_all(sampled_local, "member", split_axis=0, concat_axis=1, tiled=True)
    own_slots = lax.dynamic_slice_in_dim(obs_patch, member_index * obs_share, obs_share)
    values = sampled.astype(jnp.float32)
    obs_mean = jnp.sum(values, axis=1) / K
    spread = values - obs_mean[:, None]
    innovation = obs_values - obs_mean
    variance = jnp.sum(spread * spread, axis=1) / (K - 1)
    misfit_part = jnp.sum(innovation * innovation)
    spread_part = jnp.sum(variance + obs_errors * obs_errors)
    weighted = spread / obs_errors[:, None]
    onehot = (own_slots[None, :] == slot_table[:, None]).astype(jnp.float32)
    masked = onehot[:, :, None] * weighted[None]
    gram_own = jnp.einsum("pjk,jl->pkl", masked, weighted, precision=precise)
    cross_own = jnp.einsum("pjk,j->pk", masked, innovation / obs_errors, precision=precise)
    stacked = jnp.concatenate([gram_own, cross_own[:, None, :]], axis=1)
    summed, misfit_member, spread_member = lax.psum((stacked, misfit_part, spread_part), "member")
    numerator, denominator = lax.psum((misfit_member, spread_member), "patch")
    inflation = numerator / denominator
    rimmed = extended(summed, (("patch", 0),), 1)
    localized = rimmed[1:-1] + neighbour_weight * (rimmed[:-2] + rimmed[2:])
    gram_local = localized[:, :K]
    cross_local = localized[:, K]
    identity = jnp.eye(K, dtype=jnp.float32)
    system = (K - 1) / inflation * identity + gram_local
    root_inverse = inverse_root(system)
    inner_weights = jnp.einsum("pkl,pl->pk", root_inverse, cross_local, precision=precise)
    mean_weights = jnp.einsum("pkl,pl->pk", root_inverse, inner_weights, precision=precise)
    transform = (mean_weights[:, :, None] + math.sqrt(K - 1) * root_inverse).astype(jnp.bfloat16)
    columns = lax.all_to_all(background, "member", split_axis=1, concat_axis=3, tiled=True)
    member_mean = jnp.sum(columns.astype(jnp.float32), axis=3) / K
    anomaly = (columns.astype(jnp.float32) - member_mean[:, :, :, None, :]).astype(jnp.bfloat16)
    combined = jnp.einsum(
        "pbvlc,plk->pbvkc", anomaly, transform, preferred_element_type=jnp.float32
    )
    block_ids = member_index * block_share + jnp.arange(block_share, dtype=jnp.int32)
    in_use = (block_ids[None, :] < used_blocks[:, None])[:, :, None, None, None]
    result = jnp.where(in_use, member_mean[:, :, :, None, :] + combined, 0.0).astype(jnp.bfloat16)
    analysis = lax.all_to_all(result, "member", split_axis=3, concat_axis=1, tiled=True)
    return (analysis, inflation)


def solution(mesh):
    in_specs = (
        P("patch", None, None, "member", None),
        P(),
        P(("patch", "member")),
        P(("patch", "member")),
        P("patch"),
        P("patch"),
    )
    out_specs = (P("patch", None, None, "member", None), P())
    return jax.shard_map(
        per_device, mesh=mesh, in_specs=in_specs, out_specs=out_specs, check_vma=False
    )
```

profile of v0, /device:TPU:0, one launch (start us, length us, event | category | flops | bytes accessed | tf_op | source)
XLA Modules:
  0.0 108.1 jit_solution(4150788410182912282)
XLA Ops:
  7.2 0.0 copy-start.5
  7.2 0.0 copy-start.1
  7.2 0.0 copy-start.3
  7.2 1.0 slice_bitcast_fusion
  8.2 1.0 copy.84
  9.2 0.0 copy-done.5
  9.2 0.1 dynamic_slice.6
  9.3 0.0 copy-done.1
  9.3 0.1 select_reduce_fusion
  9.4 0.0 copy-done.3
  9.4 0.1 fusion.30
  9.6 0.0 copy-start
  9.6 6.2 %gather_fusion = bf16[2048,16]{1,0:T(8,128)(2,1)S(1)} fusion(bf16[8192,16]{1,0:T(8,128)(2,1)S(1)} %bitcast.75, s32[2048]{0:T(1024)S(1)} %fusion.30), kind=kCustom, calls=%fused_computation | custom fusion | bytes 139264 | tf_op jit(solution)/shard_map/gather | solution.py:61
  15.8 0.8 copy.85
  16.6 4.3 %all-to-all-start.1 = ((bf16[4,512,16]{1,2,0:T(8,128)(2,1)}), bf16[4,512,16]{1,2,0:T(8,128)(2,1)S(1)}, u32[]{:S(2)}, u32[]{:S(2)}) async-start(bf16[4,512,16]{1,2,0:T(8,128)(2,1)} %copy.85), calls=%async_computation.1 | async-start | bytes 131072 | tf_op jit(solution)/shard_map/all_to_all | solution.py:62
  20.8 0.1 dynamic_slice.7
  20.9 0.1 broadcast_compare_fusion
  21.0 0.0 copy-start.2
  21.0 0.0 copy-start.4
  21.0 1.0 copy.79
  22.0 2.9 %all-to-all-done.1 = bf16[4,512,16]{1,2,0:T(8,128)(2,1)S(1)} async-done(((bf16[4,512,16]{1,2,0:T(8,128)(2,1)}), bf16[4,512,16]{1,2,0:T(8,128)(2,1)S(1)}, u32[]{:S(2)}, u32[]{:S(2)}) %all-to-all-start.1) | async-done | bytes 65568 | tf_op jit(solution)/shard_map/all_to_all | solution.py:62
  25.0 3.5 %all-to-all-start = ((bf16[4,16,3,16,128]{4,3,2,0,1:T(8,128)(2,1)}), bf16[4,16,3,16,128]{4,3,2,0,1:T(8,128)(2,1)S(1)}, u32[]{:S(2)}, u32[]{:S(2)}) async-start(bf16[4,16,3,16,128]{4,3,2,0,1:T(8,128)(2,1)} %copy.79), calls=%async_computation | async-start | bytes 1572864 | tf_op jit(solution)/shard_map/all_to_all | solution.py:90
  28.5 0.0 all-reduce.4.cloned.1.call-start
  28.6 0.7 multiply_reduce_fusion.2
  29.3 0.9 fusion.7
  30.2 0.6 convolution_bitcast_fusion
  30.7 0.8 pad_maximum_fusion.2
  31.5 0.0 all-reduce.4.cloned.1.call-update
  31.5 0.1 copy.82
  31.6 0.1 copy.83
  31.7 10.3 %all-reduce.1 = (f32[]{:T(128)}, f32[]{:T(128)}) all-reduce(f32[]{:T(128)} %get-tuple-element.10, f32[]{:T(128)} %get-tuple-element.8), channel_id=1, replica_groups=mesh['patch'=8,'member'=4] {'member'}, use_global_device_ids=true, to_apply=%region_6.7 | all-reduce | flops 2 | bytes 16 | tf_op jit(solution)/shard_map/psum | solution.py:77
  42.0 22.8 %all-reduce = (f32[]{:T(128)}, f32[]{:T(128)}) all-reduce(f32[]{:T(128)} %get-tuple-element.4, f32[]{:T(128)} %get-tuple-element.5), channel_id=1, replica_groups=mesh['patch'=8,'member'=4] {'patch'}, use_global_device_ids=true, to_apply=%region_7.8 | all-reduce | flops 2 | bytes 16 | tf_op jit(solution)/shard_map/psum | solution.py:78
  66.1 0.0 all-reduce.4.cloned.1.call-done
  66.2 0.8 fusion.36
  67.0 2.8 %collective-permute-start = (f32[1,65,64]{1,2,0:T(8,128)S(1)}, f32[1,65,64]{1,2,0:T(8,128)S(1)}, u32[]{:S(2)}, u32[]{:S(2)}) collective-permute-start(f32[1,65,64]{1,2,0:T(8,128)S(1)} %get-tuple-element.6), channel_id=1, source_target_pairs={{0,4},{4,8},{8,12},{12,16},{16,20},{20,24},{24,28},{1,5},{5,9},{9,... | collective-permute-start | bytes 49928 | tf_op jit(solution)/shard_map/ppermute | solution.py:23
  69.8 1.3 %collective-permute-start.1 = (f32[1,65,64]{1,2,0:T(8,128)S(1)}, f32[1,65,64]{1,2,0:T(8,128)S(1)}, u32[]{:S(2)}, u32[]{:S(2)}) collective-permute-start(f32[1,65,64]{1,2,0:T(8,128)S(1)} %get-tuple-element.7), channel_id=1, source_target_pairs={{4,0},{8,4},{12,8},{16,12},{20,16},{24,20},{28,24},{5,1},{9,5},{13... | collective-permute-start | bytes 49928 | tf_op jit(solution)/shard_map/ppermute | solution.py:24
  71.1 0.3 collective-permute-done
  71.3 4.2 %collective-permute-done.1 = f32[1,65,64]{1,2,0:T(8,128)S(1)} collective-permute-done((f32[1,65,64]{1,2,0:T(8,128)S(1)}, f32[1,65,64]{1,2,0:T(8,128)S(1)}, u32[]{:S(2)}, u32[]{:S(2)}) %collective-permute-start.1) | collective-permute-done | bytes 16672 | tf_op jit(solution)/shard_map/ppermute | solution.py:24
  75.6 1.1 %fusion.15 = f32[4,65,64]{1,2,0:T(8,128)S(1)} fusion(f32[4,65,64]{1,2,0:T(8,128)} %all-reduce.4.cloned.1.call-done, f32[1,65,64]{1,2,0:T(8,128)S(1)} %collective-permute-done.1, f32[1,65,64]{1,2,0:T(8,128)S(1)} %collective-permute-done), kind=kLoop, calls=%fused_computation.30 | loop fusion | flops 83200 | bytes 166400 | tf_op jit(solution)/shard_map/add | solution.py:81
  76.6 0.1 multiply_reduce_fusion
  76.8 0.4 fusion.5
  77.2 0.5 fusion.33
  77.7 0.3 fusion.23
  77.9 0.3 fusion.4
  78.2 0.3 fusion.38
  78.5 0.3 fusion.37
  78.7 0.3 fusion.3
  79.0 0.3 fusion.40
  79.3 0.3 fusion.39
  79.5 0.3 fusion.2
  79.8 0.3 convolution_divide_fusion
  80.0 0.2 slice_reduce_fusion
  80.2 0.3 convolution_bitcast_fusion.1
  80.5 0.3 fusion.41
  80.9 0.0 all-to-all-done
  80.9 0.4 convert_reduce_fusion
  81.3 0.2 convert_element_type.61
  81.5 0.2 copy.89
  81.7 0.2 fusion
  81.9 0.5 fusion.1
  82.4 1.5 %copy.92 = bf16[4,4,3,64,128]{4,1,2,0,3:T(4,128)(2,1)} copy(bf16[4,4,3,64,128]{4,3,2,1,0:T(8,128)(2,1)S(1)} %fusion.1) | data formatting | bytes 1572864 | tf_op jit(solution)/shard_map/convert_element_type | solution.py:98
  83.9 3.5 %all-to-all-start.2 = ((bf16[4,4,3,64,128]{4,1,2,0,3:T(4,128)(2,1)}), bf16[4,4,3,64,128]{4,1,2,0,3:T(4,128)(2,1)S(1)}, u32[]{:S(2)}, u32[]{:S(2)}) async-start(bf16[4,4,3,64,128]{4,1,2,0,3:T(4,128)(2,1)} %copy.92), calls=%async_computation.2 | async-start | bytes 1572864 | tf_op jit(solution)/shard_map/all_to_all | solution.py:99
  88.7 10.3 %all-to-all-done.2 = bf16[4,4,3,64,128]{4,1,2,0,3:T(4,128)(2,1)S(1)} async-done(((bf16[4,4,3,64,128]{4,1,2,0,3:T(4,128)(2,1)}), bf16[4,4,3,64,128]{4,1,2,0,3:T(4,128)(2,1)S(1)}, u32[]{:S(2)}, u32[]{:S(2)}) %all-to-all-start.2) | async-done | bytes 786464 | tf_op jit(solution)/shard_map/all_to_all | solution.py:99
  99.0 1.1 %copy.93 = bf16[4,4,4,3,16,128]{5,4,3,2,1,0:T(8,128)(2,1)} copy(bf16[4,4,4,3,16,128]{5,2,3,0,4,1:T(4,128)(2,1)S(1)} %bitcast.77) | data formatting | bytes 1572864 | tf_op jit(solution)/shard_map/all_to_all | solution.py:99
  (16 shorter events, 0.2 us)
Async XLA Ops:
  7.2 2.1 %copy-start.5 = (s32[32]{0:T(128)S(1)}, s32[32]{0:T(128)}, u32[]{:S(2)}) copy-start(s32[32]{0:T(128)} %param.7) | copy-start | bytes 388
  7.2 2.1 %copy-start.1 = (s32[2048]{0:T(1024)S(1)}, s32[2048]{0:T(1024)}, u32[]{:S(2)}) copy-start(s32[2048]{0:T(1024)} %param.10) | copy-start | bytes 24580
  7.2 2.2 %copy-start.3 = (s32[2048]{0:T(1024)S(1)}, s32[2048]{0:T(1024)}, u32[]{:S(2)}) copy-start(s32[2048]{0:T(1024)} %param.11) | copy-start | bytes 24580
  9.6 11.4 %copy-start = (bf16[4,16,3,16,128]{4,3,2,1,0:T(8,128)(2,1)S(1)}, bf16[4,16,3,16,128]{4,3,2,1,0:T(8,128)(2,1)}, u32[]{:S(2)}) copy-start(bf16[4,16,3,16,128]{4,3,2,1,0:T(8,128)(2,1)} %param.6) | copy-start | bytes 2359300
  16.6 8.4 %all-to-all-start.1 = ((bf16[4,512,16]{1,2,0:T(8,128)(2,1)}), bf16[4,512,16]{1,2,0:T(8,128)(2,1)S(1)}, u32[]{:S(2)}, u32[]{:S(2)}) async-start(bf16[4,512,16]{1,2,0:T(8,128)(2,1)} %copy.85), calls=%async_computation.1 | async-start | bytes 131072 | tf_op jit(solution)/shard_map/all_to_all | solution.py:62
  21.0 7.6 %copy-start.2 = (f32[512]{0:T(512)S(1)}, f32[512]{0:T(512)}, u32[]{:S(2)}) copy-start(f32[512]{0:T(512)} %param.9) | copy-start | bytes 6148
  21.0 7.6 %copy-start.4 = (f32[512]{0:T(512)S(1)}, f32[512]{0:T(512)}, u32[]{:S(2)}) copy-start(f32[512]{0:T(512)} %param.8) | copy-start | bytes 6148
  25.0 55.9 %all-to-all-start = ((bf16[4,16,3,16,128]{4,3,2,0,1:T(8,128)(2,1)}), bf16[4,16,3,16,128]{4,3,2,0,1:T(8,128)(2,1)S(1)}, u32[]{:S(2)}, u32[]{:S(2)}) async-start(bf16[4,16,3,16,128]{4,3,2,0,1:T(8,128)(2,1)} %copy.79), calls=%async_computation | async-start | bytes 1572864 | tf_op jit(solution)/shard_map/all_to_all | solution.py:90
  28.5 37.7 %all-reduce.4.cloned.1.call-start = ((), (), s32[]{:S(2)}) async-start(), calls=%async_computation.3 | async-start | bytes 262144 | tf_op jit(solution)/shard_map/psum | solution.py:77
  67.0 4.4 %collective-permute-start = (f32[1,65,64]{1,2,0:T(8,128)S(1)}, f32[1,65,64]{1,2,0:T(8,128)S(1)}, u32[]{:S(2)}, u32[]{:S(2)}) collective-permute-start(f32[1,65,64]{1,2,0:T(8,128)S(1)} %get-tuple-element.6), channel_id=1, source_target_pairs={{0,4},{4,8},{8,12},{12,16},{16,20},{20,24},{24,28},{1,5},{5,9},{9,... | collective-permute-start | bytes 49928 | tf_op jit(solution)/shard_map/ppermute | solution.py:23
  69.8 5.8 %collective-permute-start.1 = (f32[1,65,64]{1,2,0:T(8,128)S(1)}, f32[1,65,64]{1,2,0:T(8,128)S(1)}, u32[]{:S(2)}, u32[]{:S(2)}) collective-permute-start(f32[1,65,64]{1,2,0:T(8,128)S(1)} %get-tuple-element.7), channel_id=1, source_target_pairs={{4,0},{8,4},{12,8},{16,12},{20,16},{24,20},{28,24},{5,1},{9,5},{13... | collective-permute-start | bytes 49928 | tf_op jit(solution)/shard_map/ppermute | solution.py:24
  83.9 15.1 %all-to-all-start.2 = ((bf16[4,4,3,64,128]{4,1,2,0,3:T(4,128)(2,1)}), bf16[4,4,3,64,128]{4,1,2,0,3:T(4,128)(2,1)S(1)}, u32[]{:S(2)}, u32[]{:S(2)}) async-start(bf16[4,4,3,64,128]{4,1,2,0,3:T(4,128)(2,1)} %copy.92), calls=%async_computation.2 | async-start | bytes 1572864 | tf_op jit(solution)/shard_map/all_to_all | solution.py:99
Sparse Core Ops, SparseCore 0:
  31.6 33.9 all-reduce.3
where the time goes:
time: 109 us; the launch traced here: 108 us
  blocking collectives  33.1 us (30%)
  between operations  18.1 us (17%)
  waiting for transfers between devices  17.7 us (16%)
  starting transfers between devices  15.4 us (14%)
  local copies, waits for them, and re-layouts  14.1 us (13%)
  matrix products  5.75 us (5%)
  other arithmetic  3.89 us (4%)
    psum x1, blocking collectives, per_device(): numerator, denominator = lax.psum((misfit_member, spread_member), 'patch')  22.8 us
    psum x1, blocking collectives, per_device(): lax.psum((stacked, misfit_part, spread_part), 'member')  10.3 us
    all_to_all x1, waiting for transfers between devices, per_device(): lax.all_to_all(result, 'member', split_axis=3, concat_axis=1, tiled=True)  10.3 us
    gather x1, local copies, waits for them, and re-layouts, per_device(): sampled_local = thickness[flat_index]  6.18 us
    all_to_all x1, starting transfers between devices, per_device(): lax.all_to_all(sampled_local, 'member', split_axis=0, concat_axis=1, tile...  4.26 us
    ppermute x1, waiting for transfers between devices, extended(): after = lax.ppermute(initial, axis, down)  4.23 us
    all_to_all x1, starting transfers between devices, per_device(): lax.all_to_all(background, 'member', split_axis=1, concat_axis=3, tiled=T...  3.49 us
    all_to_all x1, starting transfers between devices, per_device(): lax.all_to_all(result, 'member', split_axis=3, concat_axis=1, tiled=True)  3.49 us
  transfers between devices with their start and end apart: 6, of which 4 were waited for; matrix products, arithmetic and copies ran while one was open for 10% of the time, Pallas kernels for 0%

commit v1 on v0

--- a/solution.py
+++ b/solution.py
@@ -11,6 +11,17 @@
 PD = 4
 OBS_DEV = 2048
 neighbour_weight = 0.5
+
+
+def cut_along(value, dim, size):
+    before, after = (value.shape[:dim], value.shape[dim + 1 :])
+    return jnp.moveaxis(value.reshape(*before, size, -1, *after), dim, 0)
+
+
+def laid_out(parts, dim):
+    shape = list(parts.shape[1:])
+    shape[dim] *= parts.shape[0]
+    return jnp.moveaxis(parts, 0, dim).reshape(shape)
 
 
 def extended(array, sides, width):
@@ -96,7 +107,17 @@
     block_ids = member_index * block_share + jnp.arange(block_share, dtype=jnp.int32)
     in_use = (block_ids[None, :] < used_blocks[:, None])[:, :, None, None, None]
     result = jnp.where(in_use, member_mean[:, :, :, None, :] + combined, 0.0).astype(jnp.bfloat16)
-    analysis = lax.all_to_all(result, "member", split_axis=3, concat_axis=1, tiled=True)
+    peers, here = (lax.axis_size("member"), lax.axis_index("member"))
+    blocks = cut_along(result, 3, peers)
+    out = blocks
+    for turn in range(1, peers):
+        target, source = ((here + turn) % peers, (here - turn) % peers)
+        sent = lax.dynamic_index_in_dim(blocks, target, 0)
+        received = lax.ppermute(
+            sent, "member", [(i_2, (i_2 + turn) % peers) for i_2 in range(peers)]
+        )
+        out = lax.dynamic_update_slice_in_dim(out, received, source, axis=0)
+    analysis = laid_out(out, 1)
     return (analysis, inflation)
 
 

time: 109 us -> 103 us (0.945)
  waiting for transfers between devices: 17.7 us -> 13.5 us
  starting transfers between devices: 15.4 us -> 13.9 us
  local copies, waits for them, and re-layouts: 14.1 us -> 12.8 us
    all_to_all x1 -> x0, waiting for transfers between devices: 10.3 us -> none  [per_device(): lax.all_to_all(result, 'member', split_axis=3, concat_axis=1, tiled=True)]
    ppermute x0 -> x3, waiting for transfers between devices: none -> 6.04 us  [per_device(): lax.ppermute(sent, 'member', [(i_2, (i_2 + turn) % peers) for i_2 in rang...]
    all_to_all x1 -> x0, starting transfers between devices: 3.49 us -> none  [per_device(): lax.all_to_all(result, 'member', split_axis=3, concat_axis=1, tiled=True)]
    ppermute x0 -> x3, starting transfers between devices: none -> 2.06 us  [per_device(): lax.ppermute(sent, 'member', [(i_2, (i_2 + turn) % peers) for i_2 in rang...]
    convert_element_type x1 -> x0, local copies, waits for them, and re-layouts: 1.49 us -> none  [per_device(): jnp.where(in_use, member_mean[:, :, :, None, :] + combined, 0.0)]
  transfers between devices with their start and end apart: 6 -> 8, of which waited for: 4 -> 6; matrix products, arithmetic and copies ran while one was open for 10% -> 10% of each run, Pallas kernels for 0% -> 0%
where the time goes in v1:
time: 103 us; the launch traced here: 101 us
  blocking collectives  33.1 us (32%)
  between operations  18.2 us (18%)
  starting transfers between devices  13.9 us (13%)
  waiting for transfers between devices  13.5 us (13%)
  local copies, waits for them, and re-layouts  12.8 us (12%)
  matrix products  5.74 us (6%)
  other arithmetic  3.9 us (4%)
    psum x1, blocking collectives, per_device(): numerator, denominator = lax.psum((misfit_member, spread_member), 'patch')  22.8 us
    psum x1, blocking collectives, per_device(): lax.psum((stacked, misfit_part, spread_part), 'member')  10.3 us
    gather x1, local copies, waits for them, and re-layouts, per_device(): sampled_local = thickness[flat_index]  6.18 us
    ppermute x3, waiting for transfers between devices, per_device(): lax.ppermute(sent, 'member', [(i_2, (i_2 + turn) % peers) for i_2 in rang...  6.04 us
    all_to_all x1, starting transfers between devices, per_device(): lax.all_to_all(sampled_local, 'member', split_axis=0, concat_axis=1, tile...  4.26 us
    ppermute x1, waiting for transfers between devices, extended(): after = lax.ppermute(initial, axis, down)  4.23 us
    all_to_all x1, starting transfers between devices, per_device(): lax.all_to_all(background, 'member', split_axis=1, concat_axis=3, tiled=T...  3.49 us
    all_to_all x1, waiting for transfers between devices, per_device(): lax.all_to_all(sampled_local, 'member', split_axis=0, concat_axis=1, tile...  2.91 us
  transfers between devices with their start and end apart: 8, of which 6 were waited for; matrix products, arithmetic and copies ran while one was open for 10% of the time, Pallas kernels for 0%

profile of v1, /device:TPU:0, one launch (start us, length us, event | category | flops | bytes accessed | tf_op | source)
XLA Modules:
  0.0 101.2 jit_solution(7091995663280491514)
XLA Ops:
  7.2 1.0 slice_bitcast_fusion
  8.2 1.0 %copy.80 = bf16[4,16,128,16]{3,2,1,0:T(8,128)(2,1)S(1)} copy(bf16[4,16,128,16]{2,3,1,0:T(8,128)(2,1)S(1)} %slice_bitcast_fusion) | data formatting | bytes 524288 | tf_op jit(solution)/shard_map/transpose | solution.py:69
  9.2 0.1 dynamic_slice.16
  9.3 0.1 select_reduce_fusion
  9.4 0.1 fusion.29
  9.6 0.0 copy-start
  9.6 6.2 %gather_fusion = bf16[2048,16]{1,0:T(8,128)(2,1)S(1)} fusion(bf16[8192,16]{1,0:T(8,128)(2,1)S(1)} %bitcast.82, s32[2048]{0:T(1024)S(1)} %fusion.29), kind=kCustom, calls=%fused_computation | custom fusion | bytes 139264 | tf_op jit(solution)/shard_map/gather | solution.py:72
  15.8 0.8 copy.81
  16.6 4.3 %all-to-all-start.1 = ((bf16[4,512,16]{1,2,0:T(8,128)(2,1)}), bf16[4,512,16]{1,2,0:T(8,128)(2,1)S(1)}, u32[]{:S(2)}, u32[]{:S(2)}) async-start(bf16[4,512,16]{1,2,0:T(8,128)(2,1)} %copy.81), calls=%async_computation.1 | async-start | bytes 131072 | tf_op jit(solution)/shard_map/all_to_all | solution.py:73
  20.8 0.1 dynamic_slice.17
  20.9 0.1 broadcast_compare_fusion
  21.0 0.0 copy-done
  21.0 0.0 copy-start.2
  21.0 0.0 copy-start.4
  21.0 1.0 copy.75
  22.0 2.9 %all-to-all-done.1 = bf16[4,512,16]{1,2,0:T(8,128)(2,1)S(1)} async-done(((bf16[4,512,16]{1,2,0:T(8,128)(2,1)}), bf16[4,512,16]{1,2,0:T(8,128)(2,1)S(1)}, u32[]{:S(2)}, u32[]{:S(2)}) %all-to-all-start.1) | async-done | bytes 65568 | tf_op jit(solution)/shard_map/all_to_all | solution.py:73
  25.0 3.5 %all-to-all-start = ((bf16[4,16,3,16,128]{4,3,2,0,1:T(8,128)(2,1)}), bf16[4,16,3,16,128]{4,3,2,0,1:T(8,128)(2,1)S(1)}, u32[]{:S(2)}, u32[]{:S(2)}) async-start(bf16[4,16,3,16,128]{4,3,2,0,1:T(8,128)(2,1)} %copy.75), calls=%async_computation | async-start | bytes 1572864 | tf_op jit(solution)/shard_map/all_to_all | solution.py:101
  28.5 0.0 all-reduce.4.cloned.1.call-start
  28.6 0.0 copy-done.4
  28.6 0.7 multiply_reduce_fusion.2
  29.3 0.9 fusion.6
  30.2 0.5 convolution_bitcast_fusion
  30.7 0.8 pad_maximum_fusion.2
  31.5 0.0 all-reduce.4.cloned.1.call-update
  31.6 0.1 copy.78
  31.7 0.1 copy.79
  31.7 10.3 %all-reduce.1 = (f32[]{:T(128)}, f32[]{:T(128)}) all-reduce(f32[]{:T(128)} %get-tuple-element.13, f32[]{:T(128)} %get-tuple-element.11), channel_id=1, replica_groups=mesh['patch'=8,'member'=4] {'member'}, use_global_device_ids=true, to_apply=%region_6.7 | all-reduce | flops 2 | bytes 16 | tf_op jit(solution)/shard_map/psum | solution.py:88
  42.0 22.8 %all-reduce = (f32[]{:T(128)}, f32[]{:T(128)}) all-reduce(f32[]{:T(128)} %get-tuple-element.4, f32[]{:T(128)} %get-tuple-element.5), channel_id=1, replica_groups=mesh['patch'=8,'member'=4] {'patch'}, use_global_device_ids=true, to_apply=%region_7.8 | all-reduce | flops 2 | bytes 16 | tf_op jit(solution)/shard_map/psum | solution.py:89
  66.1 0.0 all-reduce.4.cloned.1.call-done
  66.2 0.8 fusion.35
  67.0 2.8 %collective-permute-start = (f32[1,65,64]{1,2,0:T(8,128)S(1)}, f32[1,65,64]{1,2,0:T(8,128)S(1)}, u32[]{:S(2)}, u32[]{:S(2)}) collective-permute-start(f32[1,65,64]{1,2,0:T(8,128)S(1)} %get-tuple-element.9), channel_id=1, source_target_pairs={{0,4},{4,8},{8,12},{12,16},{16,20},{20,24},{24,28},{1,5},{5,9},{9,... | collective-permute-start | bytes 49928 | tf_op jit(solution)/shard_map/ppermute | solution.py:34
  69.7 1.3 %collective-permute-start.1 = (f32[1,65,64]{1,2,0:T(8,128)S(1)}, f32[1,65,64]{1,2,0:T(8,128)S(1)}, u32[]{:S(2)}, u32[]{:S(2)}) collective-permute-start(f32[1,65,64]{1,2,0:T(8,128)S(1)} %get-tuple-element.10), channel_id=1, source_target_pairs={{4,0},{8,4},{12,8},{16,12},{20,16},{24,20},{28,24},{5,1},{9,5},{13... | collective-permute-start | bytes 49928 | tf_op jit(solution)/shard_map/ppermute | solution.py:35
  71.1 0.3 collective-permute-done
  71.3 4.2 %collective-permute-done.1 = f32[1,65,64]{1,2,0:T(8,128)S(1)} collective-permute-done((f32[1,65,64]{1,2,0:T(8,128)S(1)}, f32[1,65,64]{1,2,0:T(8,128)S(1)}, u32[]{:S(2)}, u32[]{:S(2)}) %collective-permute-start.1) | collective-permute-done | bytes 16672 | tf_op jit(solution)/shard_map/ppermute | solution.py:35
  75.6 1.1 %fusion.14 = f32[4,65,64]{1,2,0:T(8,128)S(1)} fusion(f32[4,65,64]{1,2,0:T(8,128)} %all-reduce.4.cloned.1.call-done, f32[1,65,64]{1,2,0:T(8,128)S(1)} %collective-permute-done.1, f32[1,65,64]{1,2,0:T(8,128)S(1)} %collective-permute-done), kind=kLoop, calls=%fused_computation.32 | loop fusion | flops 83200 | bytes 166400 | tf_op jit(solution)/shard_map/add | solution.py:92
  76.6 0.1 multiply_reduce_fusion
  76.8 0.4 fusion.4
  77.2 0.5 fusion.32
  77.7 0.3 fusion.22
  77.9 0.3 fusion.3
  78.2 0.3 fusion.37
  78.5 0.3 fusion.36
  78.7 0.3 fusion.2
  79.0 0.3 fusion.39
  79.3 0.3 fusion.38
  79.5 0.3 fusion.1
  79.8 0.3 convolution_divide_fusion
  80.0 0.2 slice_reduce_fusion
  80.2 0.3 convolution_bitcast_fusion.1
  80.5 0.3 fusion.40
  80.9 0.0 all-to-all-done
  80.9 0.4 convert_reduce_fusion
  81.3 0.2 convert_element_type.61
  81.5 0.2 copy.85
  81.7 0.2 fusion
  81.9 0.5 select_convert_fusion
  82.4 0.1 dynamic-slice_bitcast_fusion
  82.6 0.1 collective-permute-start.2
  82.7 0.6 collective-permute-start.3
  84.5 1.4 %collective-permute-start.4 = (bf16[1,4,4,3,16,128]{5,4,0,3,2,1:T(8,128)(2,1)S(1)}, bf16[1,4,4,3,16,128]{5,4,0,3,2,1:T(8,128)(2,1)S(1)}, u32[]{:S(2)}, u32[]{:S(2)}) collective-permute-start(bf16[1,4,4,3,16,128]{5,4,0,3,2,1:T(8,128)(2,1)S(1)} %get-tuple-element.6), channel_id=1, source_target_pairs={{0,3},{1,0},{2,1},{3,2},{4,7},{5,4},{6,5},{7,6},{8,11},{9,8},{10,9... | collective-permute-start | bytes 589832 | tf_op jit(solution)/shard_map/ppermute | solution.py:116
  86.0 3.2 %collective-permute-done.2 = bf16[1,4,4,3,16,128]{5,4,0,3,2,1:T(8,128)(2,1)S(1)} collective-permute-done((bf16[1,4,4,3,16,128]{5,4,0,3,2,1:T(8,128)(2,1)S(1)}, bf16[1,4,4,3,16,128]{5,4,0,3,2,1:T(8,128)(2,1)S(1)}, u32[]{:S(2)}, u32[]{:S(2)}) %collective-permute-start.2) | collective-permute-done | bytes 196640 | tf_op jit(solution)/shard_map/ppermute | solution.py:116
  89.2 1.3 %collective-permute-done.3 = bf16[1,4,4,3,16,128]{5,4,0,3,2,1:T(8,128)(2,1)S(1)} collective-permute-done((bf16[1,4,4,3,16,128]{5,4,0,3,2,1:T(8,128)(2,1)S(1)}, bf16[1,4,4,3,16,128]{5,4,0,3,2,1:T(8,128)(2,1)S(1)}, u32[]{:S(2)}, u32[]{:S(2)}) %collective-permute-start.3) | collective-permute-done | bytes 196640 | tf_op jit(solution)/shard_map/ppermute | solution.py:116
  90.5 1.5 %collective-permute-done.4 = bf16[1,4,4,3,16,128]{5,4,0,3,2,1:T(8,128)(2,1)S(1)} collective-permute-done((bf16[1,4,4,3,16,128]{5,4,0,3,2,1:T(8,128)(2,1)S(1)}, bf16[1,4,4,3,16,128]{5,4,0,3,2,1:T(8,128)(2,1)S(1)}, u32[]{:S(2)}, u32[]{:S(2)}) %collective-permute-start.4) | collective-permute-done | bytes 196640 | tf_op jit(solution)/shard_map/ppermute | solution.py:116
  92.1 1.1 %copy.88 = bf16[4,4,4,3,16,128]{5,4,3,2,1,0:T(8,128)(2,1)} copy(bf16[4,4,4,3,16,128]{5,4,1,3,2,0:T(8,128)(2,1)S(1)} %bitcast.86) | data formatting | bytes 1572864 | tf_op jit(solution)/shard_map/transpose | solution.py:24
  (23 shorter events, 0.3 us)
Async XLA Ops:
  7.2 2.1 %copy-start.5 = (s32[32]{0:T(128)S(1)}, s32[32]{0:T(128)}, u32[]{:S(2)}) copy-start(s32[32]{0:T(128)} %param.7) | copy-start | bytes 388
  7.2 2.1 %copy-start.1 = (s32[2048]{0:T(1024)S(1)}, s32[2048]{0:T(1024)}, u32[]{:S(2)}) copy-start(s32[2048]{0:T(1024)} %param.10) | copy-start | bytes 24580
  7.2 2.2 %copy-start.3 = (s32[2048]{0:T(1024)S(1)}, s32[2048]{0:T(1024)}, u32[]{:S(2)}) copy-start(s32[2048]{0:T(1024)} %param.11) | copy-start | bytes 24580
  9.6 11.4 %copy-start = (bf16[4,16,3,16,128]{4,3,2,1,0:T(8,128)(2,1)S(1)}, bf16[4,16,3,16,128]{4,3,2,1,0:T(8,128)(2,1)}, u32[]{:S(2)}) copy-start(bf16[4,16,3,16,128]{4,3,2,1,0:T(8,128)(2,1)} %param.6) | copy-start | bytes 2359300
  16.6 8.4 %all-to-all-start.1 = ((bf16[4,512,16]{1,2,0:T(8,128)(2,1)}), bf16[4,512,16]{1,2,0:T(8,128)(2,1)S(1)}, u32[]{:S(2)}, u32[]{:S(2)}) async-start(bf16[4,512,16]{1,2,0:T(8,128)(2,1)} %copy.81), calls=%async_computation.1 | async-start | bytes 131072 | tf_op jit(solution)/shard_map/all_to_all | solution.py:73
  21.0 7.6 %copy-start.2 = (f32[512]{0:T(512)S(1)}, f32[512]{0:T(512)}, u32[]{:S(2)}) copy-start(f32[512]{0:T(512)} %param.9) | copy-start | bytes 6148
  21.0 7.6 %copy-start.4 = (f32[512]{0:T(512)S(1)}, f32[512]{0:T(512)}, u32[]{:S(2)}) copy-start(f32[512]{0:T(512)} %param.8) | copy-start | bytes 6148
  25.0 55.9 %all-to-all-start = ((bf16[4,16,3,16,128]{4,3,2,0,1:T(8,128)(2,1)}), bf16[4,16,3,16,128]{4,3,2,0,1:T(8,128)(2,1)S(1)}, u32[]{:S(2)}, u32[]{:S(2)}) async-start(bf16[4,16,3,16,128]{4,3,2,0,1:T(8,128)(2,1)} %copy.75), calls=%async_computation | async-start | bytes 1572864 | tf_op jit(solution)/shard_map/all_to_all | solution.py:101
  28.5 37.7 %all-reduce.4.cloned.1.call-start = ((), (), s32[]{:S(2)}) async-start(), calls=%async_computation.2 | async-start | bytes 262144 | tf_op jit(solution)/shard_map/psum | solution.py:88
  67.0 4.4 %collective-permute-start = (f32[1,65,64]{1,2,0:T(8,128)S(1)}, f32[1,65,64]{1,2,0:T(8,128)S(1)}, u32[]{:S(2)}, u32[]{:S(2)}) collective-permute-start(f32[1,65,64]{1,2,0:T(8,128)S(1)} %get-tuple-element.9), channel_id=1, source_target_pairs={{0,4},{4,8},{8,12},{12,16},{16,20},{20,24},{24,28},{1,5},{5,9},{9,... | collective-permute-start | bytes 49928 | tf_op jit(solution)/shard_map/ppermute | solution.py:34
  69.7 5.8 %collective-permute-start.1 = (f32[1,65,64]{1,2,0:T(8,128)S(1)}, f32[1,65,64]{1,2,0:T(8,128)S(1)}, u32[]{:S(2)}, u32[]{:S(2)}) collective-permute-start(f32[1,65,64]{1,2,0:T(8,128)S(1)} %get-tuple-element.10), channel_id=1, source_target_pairs={{4,0},{8,4},{12,8},{16,12},{20,16},{24,20},{28,24},{5,1},{9,5},{13... | collective-permute-start | bytes 49928 | tf_op jit(solution)/shard_map/ppermute | solution.py:35
  82.6 6.6 %collective-permute-start.2 = (bf16[1,4,4,3,16,128]{5,4,0,3,2,1:T(8,128)(2,1)S(1)}, bf16[1,4,4,3,16,128]{5,4,0,3,2,1:T(8,128)(2,1)S(1)}, u32[]{:S(2)}, u32[]{:S(2)}) collective-permute-start(bf16[1,4,4,3,16,128]{5,4,0,3,2,1:T(8,128)(2,1)S(1)} %get-tuple-element.8), channel_id=1, source_target_pairs={{0,1},{1,2},{2,3},{3,0},{4,5},{5,6},{6,7},{7,4},{8,9},{9,10},{10,1... | collective-permute-start | bytes 589832 | tf_op jit(solution)/shard_map/ppermute | solution.py:116
  82.7 7.8 %collective-permute-start.3 = (bf16[1,4,4,3,16,128]{5,4,0,3,2,1:T(8,128)(2,1)S(1)}, bf16[1,4,4,3,16,128]{5,4,0,3,2,1:T(8,128)(2,1)S(1)}, u32[]{:S(2)}, u32[]{:S(2)}) collective-permute-start(bf16[1,4,4,3,16,128]{5,4,0,3,2,1:T(8,128)(2,1)S(1)} %get-tuple-element.7), channel_id=1, source_target_pairs={{0,2},{1,3},{2,0},{3,1},{4,6},{5,7},{6,4},{7,5},{8,10},{9,11},{10,... | collective-permute-start | bytes 589832 | tf_op jit(solution)/shard_map/ppermute | solution.py:116
  84.5 7.5 %collective-permute-start.4 = (bf16[1,4,4,3,16,128]{5,4,0,3,2,1:T(8,128)(2,1)S(1)}, bf16[1,4,4,3,16,128]{5,4,0,3,2,1:T(8,128)(2,1)S(1)}, u32[]{:S(2)}, u32[]{:S(2)}) collective-permute-start(bf16[1,4,4,3,16,128]{5,4,0,3,2,1:T(8,128)(2,1)S(1)} %get-tuple-element.6), channel_id=1, source_target_pairs={{0,3},{1,0},{2,1},{3,2},{4,7},{5,4},{6,5},{7,6},{8,11},{9,8},{10,9... | collective-permute-start | bytes 589832 | tf_op jit(solution)/shard_map/ppermute | solution.py:116
Sparse Core Ops, SparseCore 0:
  31.6 33.9 all-reduce.3
